TPU v7x, 32 devices: a whole 2x2x4 slice. The times are simulated.
32 devices in a mesh: section: 4 (over y, x), ctx: 4 (over z), mp: 2 (over core).
Axes of the slice: x: 2, y: 2, z: 4, core: 2. Of those that a mesh axis runs over, the one named last changes fastest.
Arguments:
- head_input: bfloat16 [4, 1024, 2048], P('section', 'ctx', 'mp'), may hold values from -6 to 6
- state_proj: bfloat16 [4, 1024, 256], P('section', 'ctx'), may hold values from -6 to 6
- gate_input: bfloat16 [4, 1024, 2048], P('section', 'ctx', 'mp'), may hold values from -6 to 6
- step_raw: float32 [4, 32, 1024], P('section', 'mp', 'ctx'), may hold values from -2 to 2
- step_bias: float32 [4, 32], P('section', 'mp'), may hold values from -9.5 to -3
- decay_log: float32 [4, 32], P('section', 'mp'), may hold values from -7 to 1.5
- skip_gain: float32 [4, 32], P('section', 'mp'), may hold values from 0.5 to 1.5
- conv_head: float32 [4, 4, 2048], P('section', None, 'mp'), may hold values from -3 to 3
- conv_state: float32 [4, 4, 256], P('section'), may hold values from -3 to 3
- norm_gain: float32 [4, 2048], P('section', 'mp'), may hold values from 0.1 to 1.9
- next_weight: bfloat16 [4, 2048, 4096], P('section', 'ctx', 'mp'), may hold values from -0.125 to 0.125
Outputs:
- projected: bfloat16 [4, 1024, 4096], P('section', 'ctx', 'mp')
All inputs are finite; a program needn't handle non-finite values.
Results may differ from a plain program's by a relative error of at most 0.0087.
Values may be sent and summed in bfloat16 or wider, within the bound.
A program may use at most 64 MiB of HBM per device.

v0:
```python
import jax
import jax.numpy as jnp
from jax import lax
from jax.sharding import PartitionSpec as P

STATE = 128
BLOCK = 256
FEATURES = 2048
NORM_FLOOR = 0.25
HIGHEST = lax.Precision.HIGHEST


def from_behind(value, axis, steps):
    count = lax.axis_size(axis)
    first, last = (max(0, -steps), min(count, count - steps))
    return lax.ppermute(value, axis, [(source, source + steps) for source in range(first, last)])


def prefix(part, axis, combine, identity):
    place = lax.axis_index(axis)
    gathered = jax.tree.map(lambda a: lax.all_gather(a, axis), part)
    state = jax.tree.map(lambda a, e: jnp.zeros_like(a) + jnp.asarray(e, a.dtype), part, identity)

    def one(step, state):
        return combine(
            state, jax.tree.map(lambda a: lax.dynamic_index_in_dim(a, step, 0, False), gathered)
        )

    return lax.fori_loop(0, place, one, state)


def shifted(value, axis, steps):
    count = lax.axis_size(axis)
    pairs = [(source, (source + steps) % count) for source in range(count)]
    return lax.ppermute(value, axis, pairs)


def causal_conv(sequence, previous, weights):
    length = sequence.shape[0]
    padded = jnp.concatenate([previous, sequence], axis=0).astype(jnp.float32)
    summed = jnp.zeros(sequence.shape, jnp.float32)
    for offset in range(weights.shape[0]):
        summed = summed + weights[offset] * padded[offset : offset + length]
    return summed


def chain_step(earlier, latter):
    return (earlier[0] + latter[0], jnp.exp(latter[0])[:, None, None] * earlier[1] + latter[1])


def shards(
    head_input,
    state_proj,
    gate_input,
    step_raw,
    step_bias,
    decay_log,
    skip_gain,
    conv_head,
    conv_state,
    norm_gain,
    next_weight,
):
    tap_count = conv_head.shape[1]
    token_count = head_input.shape[1]
    local_width = head_input.shape[2]
    head_count = step_raw.shape[1]
    head_width = local_width // head_count
    block_count = token_count // BLOCK
    tails = jnp.concatenate(
        [
            head_input[0, token_count - tap_count + 1 :],
            state_proj[0, token_count - tap_count + 1 :],
        ],
        axis=1,
    )
    previous = from_behind(tails, "ctx", 1)
    conv_x = jax.nn.silu(
        causal_conv(head_input[0], previous[:, :local_width], conv_head[0])
    ).astype(jnp.bfloat16)
    conv_bc = causal_conv(state_proj[0], previous[:, local_width:], conv_state[0]).astype(
        jnp.bfloat16
    )
    blocks_x = conv_x.reshape(block_count, BLOCK, head_count, head_width)
    blocks_b = conv_bc[:, :STATE].reshape(block_count, BLOCK, STATE)
    blocks_c = conv_bc[:, STATE:].reshape(block_count, BLOCK, STATE)
    step_size = jax.nn.softplus(step_raw[0] + step_bias[0][:, None])
    log_decay = -jnp.exp(decay_log[0])[:, None] * step_size
    blocks_step = step_size.reshape(head_count, block_count, BLOCK)
    blocks_decay = log_decay.reshape(head_count, block_count, BLOCK)
    row_index = lax.broadcasted_iota(jnp.int32, (BLOCK, BLOCK), 0)
    col_index = lax.broadcasted_iota(jnp.int32, (BLOCK, BLOCK), 1)
    causal_mask = row_index >= col_index
    lower_tri = causal_mask.astype(jnp.float32)
    cumulative = jnp.einsum("hcs,ts->hct", blocks_decay, lower_tri, precision=HIGHEST)
    scores = jnp.einsum("ctn,csn->cts", blocks_c, blocks_b, preferred_element_type=jnp.float32)
    decay_diff = jnp.where(causal_mask, cumulative[..., :, None] - cumulative[..., None, :], 0.0)
    mix_weight = jnp.where(
        causal_mask, scores[None] * jnp.exp(decay_diff) * blocks_step[:, :, None, :], 0.0
    ).astype(jnp.bfloat16)
    intra_part = jnp.einsum(
        "hcts,cshp->cthp", mix_weight, blocks_x, preferred_element_type=jnp.float32
    )
    tail_weight = jnp.exp(cumulative[..., -1:] - cumulative) * blocks_step
    weighted_b = (blocks_b.astype(jnp.float32)[None] * tail_weight[..., None]).astype(jnp.bfloat16)
    updates = jnp.einsum(
        "cshp,hcsn->chpn", blocks_x, weighted_b, preferred_element_type=jnp.float32
    )
    totals = cumulative[..., -1]
    running = jnp.zeros((head_count, head_width, STATE), jnp.float32)
    before = jnp.zeros((head_count,), jnp.float32)
    entering = running
    offsets = before
    running = jnp.exp(totals[:, 0])[:, None, None] * running + updates[0]
    before = totals[:, 0]
    prior_log, prior_state = prefix(
        (before, running), "ctx", chain_step, (jnp.zeros_like(before), jnp.zeros_like(running))
    )
    full_states = jnp.stack([entering + jnp.exp(offsets)[:, None, None] * prior_state])
    inter_part = (
        jnp.einsum("ctn,chpn->cthp", blocks_c.astype(jnp.float32), full_states, precision=HIGHEST)
        * jnp.exp(cumulative).transpose(1, 2, 0)[..., None]
    )
    output = (
        intra_part + inter_part + skip_gain[0][None, None, :, None] * blocks_x.astype(jnp.float32)
    )
    gated = output.reshape(token_count, local_width) * jax.nn.silu(
        gate_input[0].astype(jnp.float32)
    )
    squares = lax.psum(jnp.sum(gated * gated, axis=1), "mp")
    mean_square = squares / FEATURES
    normed = (gated * lax.rsqrt(mean_square + NORM_FLOOR)[:, None] * norm_gain[0][None]).astype(
        jnp.bfloat16
    )
    gathered = lax.all_gather(normed, "mp", axis=1, tiled=True)
    arrived = shifted(gathered, "section", 1)
    weight_rows = next_weight[0]
    full_weight = lax.all_gather(weight_rows, "ctx", axis=0, tiled=True)
    result = jnp.dot(arrived, full_weight, preferred_element_type=jnp.float32)
    return result.astype(jnp.bfloat16)[None]


def solution(mesh):
    return jax.shard_map(
        shards,
        mesh=mesh,
        in_specs=(
            P("section", "ctx", "mp"),
            P("section", "ctx", None),
            P("section", "ctx", "mp"),
            P("section", "mp", "ctx"),
            P("section", "mp"),
            P("section", "mp"),
            P("section", "mp"),
            P("section", None, "mp"),
            P("section", None, None),
            P("section", "mp"),
            P("section", "ctx", "mp"),
        ),
        out_specs=P("section", "ctx", "mp"),
        check_vma=False,
    )
```

profile of v0, /device:TPU:0, one launch (start us, length us, event | category | flops | bytes accessed | tf_op | source)
XLA Modules:
  0.0 252.9 jit_solution(13187980075487507299)
XLA Ops:
  6.5 0.7 slice_bitcast_fusion
  7.3 0.7 slice_bitcast_fusion.1
  8.0 5.0 %collective-permute-start = (bf16[3,1280]{1,0:T(4,128)(2,1)S(1)}, bf16[3,1280]{1,0:T(4,128)(2,1)S(1)}, u32[]{:S(2)}, u32[]{:S(2)}) collective-permute-start(bf16[3,1280]{1,0:T(4,128)(2,1)S(1)} %pad_maximum_fusion), channel_id=1, source_target_pairs={{0,2},{2,4},{4,6},{1,3},{3,5},{5,7},{8,10},{10,12},{12,14},{9,11},... | collective-permute-start | bytes 23048 | tf_op jit(solution)/shard_map/ppermute | solution.py:16
  12.9 0.9 fusion.44
  13.8 0.7 negate_bitcast_fusion
  14.5 0.8 compare_select_fusion
  15.3 0.2 fusion.35
  15.5 0.3 multiply_reduce_fusion.1
  15.7 0.8 exponential_bitcast_fusion.1
  16.6 0.8 fusion.45
  17.4 1.2 copy.20
  18.7 0.2 copy.21
  18.9 0.9 maximum_convert_fusion.1
  20.0 0.4 maximum_convert_fusion
  20.4 1.6 multiply_convert_fusion.2
  22.0 1.6 convolution_add_fusion
  23.7 0.7 dynamic-slice
  25.0 0.2 dynamic-update-slice
  25.3 10.0 %all-reduce = f32[64]{0:T(128)S(1)} all-reduce(f32[64]{0:T(128)S(1)} %dynamic-update-slice), channel_id=2, replica_groups=mesh['section'=4,'ctx'=4,'mp'=2] {'ctx'}, use_global_device_ids=true, to_apply=%add | all-reduce | flops 64 | bytes 512
  35.4 0.2 copy.22
  35.7 0.2 fusion.37
  35.8 33.8 %all-gather.9.cloned.1.call-done = f32[64,64,128]{2,1,0:T(8,128)} async-done(((f32[16,64,128]{2,1,0:T(8,128)}), f32[64,64,128]{2,1,0:T(8,128)}) %all-gather.9.cloned.1.call-update) | async-done | bytes 2097168 | tf_op jit(solution)/shard_map/all_gather | solution.py:21
  69.8 0.6 fusion.16
  70.4 1.6 multiply_reduce_fusion
  72.0 2.5 psum.7
  74.5 1.2 fusion.30
  75.7 0.7 all-gather.11.cloned.1.call-update
  76.4 10.9 %all-gather.7.cloned.1.call-done = bf16[256,2048]{0,1:T(8,128)(2,1)} async-done(((bf16[256,1024]{0,1:T(8,128)(2,1)}), bf16[256,2048]{0,1:T(8,128)(2,1)}) %all-gather.7.cloned.1.call-update) | async-done | bytes 1048592 | tf_op jit(solution)/shard_map/all_gather | solution.py:135
  87.3 1.7 collective-permute-start.1
  89.0 24.7 %collective-permute-done.1 = bf16[256,2048]{0,1:T(8,128)(2,1)S(1)} collective-permute-done((bf16[256,2048]{0,1:T(8,128)(2,1)}, bf16[256,2048]{0,1:T(8,128)(2,1)S(1)}, u32[]{:S(2)}, u32[]{:S(2)}) %collective-permute-start.1) | collective-permute-done | bytes 1048608 | tf_op jit(solution)/shard_map/ppermute | solution.py:35
  113.8 125.9 %all-gather.11.cloned.1.call-done = bf16[1,2048,2048]{2,1,0:T(8,128)(2,1)} async-done(((bf16[1,512,2048]{2,1,0:T(8,128)(2,1)}), bf16[1,2048,2048]{2,1,0:T(8,128)(2,1)}) %all-gather.11.cloned.1.call-update) | async-done | bytes 8388624 | tf_op jit(solution)/shard_map/all_gather | solution.py:138
  239.7 6.7 %fusion.5 = bf16[1,256,2048]{2,1,0:T(8,128)(2,1)} fusion(bf16[256,2048]{0,1:T(8,128)(2,1)S(1)} %collective-permute-done.1, bf16[1,2048,2048]{2,1,0:T(8,128)(2,1)} %all-gather.11.cloned.1.call-done), kind=kOutput, calls=%fused_computation.6 | convolution fusion | flops 2148007936 | bytes 10485760 | tf_op jit(solution)/shard_map/dot_general | solution.py:139
  (25 shorter events, 0.5 us)
Async XLA Ops:
  6.5 63.1 %all-gather.9.cloned.1.call-start = ((), (), s32[]{:S(2)}) async-start(), calls=%async_computation.1 | async-start | bytes 2621440 | tf_op jit(solution)/shard_map/all_gather | solution.py:21
  8.0 10.7 %collective-permute-start = (bf16[3,1280]{1,0:T(4,128)(2,1)S(1)}, bf16[3,1280]{1,0:T(4,128)(2,1)S(1)}, u32[]{:S(2)}, u32[]{:S(2)}) collective-permute-start(bf16[3,1280]{1,0:T(4,128)(2,1)S(1)} %pad_maximum_fusion), channel_id=1, source_target_pairs={{0,2},{2,4},{4,6},{1,3},{3,5},{5,7},{8,10},{10,12},{12,14},{9,11},... | collective-permute-start | bytes 23048 | tf_op jit(solution)/shard_map/ppermute | solution.py:16
  20.0 3.7 %copy-start.3 = (u32[32]{0:T(128)S(1)}, u32[32]{0:T(128)}, u32[]{:S(2)}) copy-start(u32[32]{0:T(128)} %constant.51) | copy-start | bytes 388
  20.0 15.4 %copy-start = (bf16[1,256,1024]{2,1,0:T(8,128)(2,1)S(1)}, bf16[1,256,1024]{2,1,0:T(8,128)(2,1)}, u32[]{:S(2)}) copy-start(bf16[1,256,1024]{2,1,0:T(8,128)(2,1)} %param.15) | copy-start | bytes 1572868
  23.6 63.7 %all-gather.7.cloned.1.call-start = ((), (), s32[]{:S(2)}) async-start(), calls=%async_computation | async-start | bytes 1572864 | tf_op jit(solution)/shard_map/all_gather | solution.py:135
  69.7 0.7 copy-start.2
  70.4 4.1 %copy-start.1 = (f32[1,1024]{1,0:T(1,128)S(1)}, f32[1,1024]{1,0:T(1,128)}, u32[]{:S(2)}) copy-start(f32[1,1024]{1,0:T(1,128)} %param.22) | copy-start | bytes 12292
  75.7 164.0 %all-gather.11.cloned.1.call-start = ((), (), s32[]{:S(2)}) async-start(), calls=%async_computation.2 | async-start | bytes 10485760 | tf_op jit(solution)/shard_map/all_gather | solution.py:138
  87.3 26.5 %collective-permute-start.1 = (bf16[256,2048]{0,1:T(8,128)(2,1)}, bf16[256,2048]{0,1:T(8,128)(2,1)S(1)}, u32[]{:S(2)}, u32[]{:S(2)}) collective-permute-start(bf16[256,2048]{0,1:T(8,128)(2,1)} %all-gather.7.cloned.1.call-done), channel_id=1, source_target_pairs={{0,8},{8,16},{16,24},{24,0},{1,9},{9,17},{17,25},{25,1},{2,10},{10... | collective-permute-start | bytes 3145736 | tf_op jit(solution)/shard_map/ppermute | solution.py:35
Sparse Core Ops, SparseCore 0:
  23.7 45.8 all-gather.8
  75.8 11.4 all-gather.6
  88.9 150.7 all-gather.10
where the time goes:
time: 254 us; the launch traced here: 253 us
  waiting for transfers between devices  196 us (77%)
  between operations  14 us (6%)
  blocking collectives  12.5 us (5%)
  matrix products  10.9 us (4%)
  other arithmetic  6.79 us (3%)
  starting transfers between devices  6.78 us (3%)
  local copies, waits for them, and re-layouts  5.88 us (2%)
    all_gather x1, waiting for transfers between devices, shards(): full_weight = lax.all_gather(weight_rows, 'ctx', axis=0, tiled=True)  126 us
    all_gather x1, waiting for transfers between devices, prefix(): gathered = jax.tree.map(lambda a: lax.all_gather(a, axis), part)  33.8 us
    ppermute x1, waiting for transfers between devices, shifted(): return lax.ppermute(value, axis, pairs)  24.7 us
    all_gather x1, waiting for transfers between devices, shards(): gathered = lax.all_gather(normed, 'mp', axis=1, tiled=True)  10.9 us
    unnamed x1, blocking collectives  10 us
    dot_general x1, matrix products, shards(): result = jnp.dot(arrived, full_weight, preferred_element_type=jnp.float32)  6.7 us
  transfers between devices with their start and end apart: 5, of which 4 were waited for; matrix products, arithmetic and copies ran while one was open for 3% of the time, Pallas kernels for 0%

commit v1 on v0

--- a/solution.py
+++ b/solution.py
@@ -135,7 +135,12 @@
     gathered = lax.all_gather(normed, "mp", axis=1, tiled=True)
     arrived = shifted(gathered, "section", 1)
     weight_rows = next_weight[0]
-    full_weight = lax.all_gather(weight_rows, "ctx", axis=0, tiled=True)
+    ring = [weight_rows]
+    for hop in range(3):
+        ring.append(lax.ppermute(ring[-1], "ctx", [(dev, (dev + 1) % 4) for dev in range(4)]))
+    full_weight = jnp.roll(
+        jnp.concatenate(ring[::-1], axis=0), (lax.axis_index("ctx") + 1) * ring[0].shape[0], axis=0
+    )
     result = jnp.dot(arrived, full_weight, preferred_element_type=jnp.float32)
     return result.astype(jnp.bfloat16)[None]
 

time: 254 us -> 236 us (0.929)
  waiting for transfers between devices: 196 us -> 118 us
  blocking collectives: 12.5 us -> 51.1 us
  local copies, waits for them, and re-layouts: 5.88 us -> 19.1 us
  starting transfers between devices: 6.78 us -> 12.2 us
  other arithmetic: 6.79 us -> 10.7 us
    all_gather x1 -> x0, waiting for transfers between devices: 126 us -> none  [shards(): full_weight = lax.all_gather(weight_rows, 'ctx', axis=0, tiled=True)]
    ppermute x0 -> x3, waiting for transfers between devices: none -> 107 us  [shards(): lax.ppermute(ring[-1], 'ctx', [(dev, (dev + 1) % 4) for dev in range(4)])]
    unnamed x1, blocking collectives: 10 us -> 48.7 us
    all_gather x1, waiting for transfers between devices: 33.8 us -> 0.02 us  [prefix(): gathered = jax.tree.map(lambda a: lax.all_gather(a, axis), part)]
    ppermute x1, waiting for transfers between devices: 24.7 us -> 0.01 us  [shifted(): return lax.ppermute(value, axis, pairs)]
    unnamed x13 -> x34, local copies, waits for them, and re-layouts: 2.39 us -> 14.3 us
    ppermute x0 -> x3, starting transfers between devices: none -> 5.44 us  [shards(): lax.ppermute(ring[-1], 'ctx', [(dev, (dev + 1) % 4) for dev in range(4)])]
    dot_general x1, matrix products: 6.7 us -> 3.32 us  [shards(): result = jnp.dot(arrived, full_weight, preferred_element_type=jnp.float32)]
  transfers between devices with their start and end apart: 5 -> 7, of which waited for: 4 -> 3; matrix products, arithmetic and copies ran while one was open for 3% -> 12% of each run, Pallas kernels for 0% -> 0%
where the time goes in v1:
time: 236 us; the launch traced here: 235 us
  waiting for transfers between devices  118 us (50%)
  blocking collectives  51.1 us (22%)
  local copies, waits for them, and re-layouts  19.1 us (8%)
  between operations  14.4 us (6%)
  starting transfers between devices  12.2 us (5%)
  other arithmetic  10.7 us (5%)
  matrix products  9.68 us (4%)
    ppermute x3, waiting for transfers between devices, shards(): lax.ppermute(ring[-1], 'ctx', [(dev, (dev + 1) % 4) for dev in range(4)])  107 us
    unnamed x1, blocking collectives  48.7 us
    unnamed x34, local copies, waits for them, and re-layouts  14.3 us
    all_gather x1, waiting for transfers between devices, shards(): gathered = lax.all_gather(normed, 'mp', axis=1, tiled=True)  11.2 us
    ppermute x3, starting transfers between devices, shards(): lax.ppermute(ring[-1], 'ctx', [(dev, (dev + 1) % 4) for dev in range(4)])  5.44 us
    ppermute x1, starting transfers between devices, from_behind(): lax.ppermute(value, axis, [(source, source + steps) for source in range(f...  4.96 us
  transfers between devices with their start and end apart: 7, of which 3 were waited for; matrix products, arithmetic and copies ran while one was open for 12% of the time, Pallas kernels for 0%

profile of v1, /device:TPU:0, one launch (start us, length us, event | category | flops | bytes accessed | tf_op | source)
XLA Modules:
  0.0 235.1 jit_solution(10748900070266905472)
XLA Ops:
  6.5 0.7 slice_bitcast_fusion.1
  7.2 0.7 slice_bitcast_fusion
  8.0 5.0 %collective-permute-start = (bf16[3,1280]{1,0:T(4,128)(2,1)S(1)}, bf16[3,1280]{1,0:T(4,128)(2,1)S(1)}, u32[]{:S(2)}, u32[]{:S(2)}) collective-permute-start(bf16[3,1280]{1,0:T(4,128)(2,1)S(1)} %pad_maximum_fusion), channel_id=1, source_target_pairs={{0,2},{2,4},{4,6},{1,3},{3,5},{5,7},{8,10},{10,12},{12,14},{9,11},... | collective-permute-start | bytes 23048 | tf_op jit(solution)/shard_map/ppermute | solution.py:16
  13.6 0.8 compare_select_fusion
  14.6 0.8 multiply_reduce_fusion.1
  15.5 1.5 fusion.45
  16.9 1.4 exponential_bitcast_fusion.1
  18.4 0.8 fusion.46
  19.2 1.2 copy.20
  20.7 0.9 maximum_convert_fusion.1
  22.2 2.5 %multiply_convert_fusion.2 = bf16[256,1024]{0,1:T(8,128)(2,1)S(1)} fusion(f32[259,1024]{0,1:T(8,128)S(1)} %maximum_convert_fusion, f32[1024]{0:T(1024)} %bitcast.103, f32[1024]{0:T(1024)} %bitcast.104, f32[1024]{0:T(1024)} %bitcast.102, f32[1024]{0:T(1024)} %bitcast.101), kind=kLoop, calls=%fused_computation.40 | loop fusion | flops 3145728 | bytes 4734976 | tf_op jit(solution)/shard_map/convert_element_type | solution.py:80
  24.8 0.8 copy-done.1
  25.6 1.6 convolution_add_fusion
  27.3 1.6 collective-permute-start.2
  28.9 81.2 %collective-permute-done.2 = bf16[512,2048]{1,0:T(8,128)(2,1)} collective-permute-done((bf16[512,2048]{1,0:T(8,128)(2,1)S(1)}, bf16[512,2048]{1,0:T(8,128)(2,1)}, u32[]{:S(2)}, u32[]{:S(2)}) %collective-permute-start.2) | collective-permute-done | bytes 2097184 | tf_op jit(solution)/shard_map/ppermute | solution.py:140
  110.1 0.7 dynamic-slice
  111.7 48.7 %all-reduce = f32[64]{0:T(128)S(1)} all-reduce(f32[64]{0:T(128)S(1)} %dynamic-update-slice), channel_id=2, replica_groups=mesh['section'=4,'ctx'=4,'mp'=2] {'ctx'}, use_global_device_ids=true, to_apply=%add | all-reduce | flops 64 | bytes 512
  160.4 0.7 reshape.203
  162.8 3.8 %collective-permute-start.4 = (bf16[512,2048]{1,0:T(8,128)(2,1)}, bf16[512,2048]{1,0:T(8,128)(2,1)}, u32[]{:S(2)}, u32[]{:S(2)}) collective-permute-start(bf16[512,2048]{1,0:T(8,128)(2,1)} %collective-permute-done.3), channel_id=1, source_target_pairs={{0,2},{2,4},{4,6},{6,0},{1,3},{3,5},{5,7},{7,1},{8,10},{10,12},{12... | collective-permute-start | bytes 6291464 | tf_op jit(solution)/shard_map/ppermute | solution.py:140
  166.7 3.8 %multiply_reduce_fusion = (f32[256]{0:T(256)S(1)}, f32[1,256,16,64]{1,3,2,0:T(8,128)}) fusion(bf16[1,256,16,64]{1,3,2,0:T(8,128)(2,1)} %bitcast.98, f32[16]{0:T(128)} %bitcast.112, f32[1,256,16,64]{1,3,2,0:T(8,128)S(1)} %fusion.16, bf16[256,16,64]{0,2,1:T(8,128)(2,1)} %bitcast.97, f32[16,256]{1,0:T(8,128)} %copy-done.4, f32[16,256]{1,0:T(8,128)} %copy-done.3, ...), kind=kOutput, calls=%fused_computation.37 | convolution fusion | flops 143654656 | bytes 4031552 | tf_op jit(solution)/shard_map/hcts,cshp->cthp/dot_general | solution.py:101
  170.4 2.4 %psum.7 = f32[256]{0:T(256)S(1)} all-reduce(f32[256]{0:T(256)S(1)} %get-tuple-element.72), channel_id=1, replica_groups=mesh['section'=4,'ctx'=4,'mp'=2] {'mp'}, use_global_device_ids=true, to_apply=%region_3.4 | all-reduce | flops 256 | bytes 2048 | tf_op jit(solution)/shard_map/psum | solution.py:130
  172.9 2.4 %fusion.30 = bf16[256,1024]{0,1:T(8,128)(2,1)} fusion(f32[1,256,16,64]{1,3,2,0:T(8,128)} %get-tuple-element.73, f32[1024]{0:T(1024)S(1)} %bitcast.105, f32[256]{0:T(256)S(1)} %add_rsqrt_fusion, bf16[1,256,1024]{1,2,0:T(8,128)(2,1)S(1)} %copy.22), kind=kLoop, calls=%fused_computation.41 | loop fusion | flops 2359296 | bytes 2102272 | tf_op jit(solution)/shard_map/convert_element_type | solution.py:132
  175.3 11.2 %all-gather.5.cloned.1.call-done = bf16[256,2048]{0,1:T(8,128)(2,1)} async-done(((bf16[256,1024]{0,1:T(8,128)(2,1)}), bf16[256,2048]{0,1:T(8,128)(2,1)}) %all-gather.5.cloned.1.call-update) | async-done | bytes 1048592 | tf_op jit(solution)/shard_map/all_gather | solution.py:135
  186.5 1.7 collective-permute-start.1
  188.2 25.4 %collective-permute-done.4 = bf16[512,2048]{1,0:T(8,128)(2,1)} collective-permute-done((bf16[512,2048]{1,0:T(8,128)(2,1)}, bf16[512,2048]{1,0:T(8,128)(2,1)}, u32[]{:S(2)}, u32[]{:S(2)}) %collective-permute-start.4) | collective-permute-done | bytes 2097184 | tf_op jit(solution)/shard_map/ppermute | solution.py:140
  213.6 1.8 constant_dynamic-update-slice_fusion.7
  215.4 1.8 constant_dynamic-update-slice_fusion.6
  217.3 1.8 constant_dynamic-update-slice_fusion.5
  219.3 1.8 constant_dynamic-update-slice_fusion.3
  221.1 1.8 constant_dynamic-update-slice_fusion.2
  222.9 1.8 constant_dynamic-update-slice_fusion.1
  224.9 3.3 %fusion.5 = bf16[1,256,2048]{2,1,0:T(8,128)(2,1)} fusion(bf16[256,2048]{0,1:T(8,128)(2,1)S(1)} %collective-permute-done.1, bf16[4096,2048]{1,0:T(8,128)(2,1)S(1)} %constant_dynamic-update-slice_fusion, s32[]{:T(128)S(6)} %select_n.46), kind=kOutput, calls=%fused_computation.6 | convolution fusion | flops 2148007936 | bytes 10485764 | tf_op jit(solution)/shard_map/dot_general | solution.py:144
  (50 shorter events, 3.9 us)
Async XLA Ops:
  6.5 155.6 %all-gather.7.cloned.1.call-start = ((), (), s32[]{:S(2)}) async-start(), calls=%async_computation.1 | async-start | bytes 2621440 | tf_op jit(solution)/shard_map/all_gather | solution.py:21
  8.0 12.5 %collective-permute-start = (bf16[3,1280]{1,0:T(4,128)(2,1)S(1)}, bf16[3,1280]{1,0:T(4,128)(2,1)S(1)}, u32[]{:S(2)}, u32[]{:S(2)}) collective-permute-start(bf16[3,1280]{1,0:T(4,128)(2,1)S(1)} %pad_maximum_fusion), channel_id=1, source_target_pairs={{0,2},{2,4},{4,6},{1,3},{3,5},{5,7},{8,10},{10,12},{12,14},{9,11},... | collective-permute-start | bytes 23048 | tf_op jit(solution)/shard_map/ppermute | solution.py:16
  14.4 7.4 %copy-start.4 = (f32[16,256]{1,0:T(8,128)}, f32[16,256]{1,0:T(8,128)S(1)}, u32[]{:S(2)}) copy-start(f32[16,256]{1,0:T(8,128)S(1)} %compare_select_fusion) | copy-start | bytes 49156
  14.6 7.2 %copy-start.3 = (f32[16,256]{1,0:T(8,128)}, f32[16,256]{1,0:T(8,128)S(1)}, u32[]{:S(2)}) copy-start(f32[16,256]{1,0:T(8,128)S(1)} %fusion.35) | copy-start | bytes 49156
  15.5 6.4 %copy-start.7 = (f32[16]{0:T(128)}, f32[16]{0:T(128)S(1)}, u32[]{:S(2)}) copy-start(f32[16]{0:T(128)S(1)} %get-tuple-element.51) | copy-start | bytes 196
  21.6 3.9 %copy-start.5 = (f32[16,256]{1,0:T(8,128)S(1)}, f32[16,256]{1,0:T(8,128)}, u32[]{:S(2)}) copy-start(f32[16,256]{1,0:T(8,128)} %get-tuple-element.63) | copy-start | bytes 49156
  21.7 3.9 %copy-start.9 = (f32[16]{0:T(128)S(1)}, f32[16]{0:T(128)}, u32[]{:S(2)}) copy-start(f32[16]{0:T(128)} %get-tuple-element.50) | copy-start | bytes 196
  21.8 5.4 %copy-start = (bf16[1,512,2048]{2,1,0:T(8,128)(2,1)S(1)}, bf16[1,512,2048]{2,1,0:T(8,128)(2,1)}, u32[]{:S(2)}) copy-start(bf16[1,512,2048]{2,1,0:T(8,128)(2,1)} %param.23) | copy-start | bytes 6291460
  21.9 139.2 %copy-start.2 = (bf16[1,256,1024]{2,1,0:T(8,128)(2,1)S(1)}, bf16[1,256,1024]{2,1,0:T(8,128)(2,1)}, u32[]{:S(2)}) copy-start(bf16[1,256,1024]{2,1,0:T(8,128)(2,1)} %param.15) | copy-start | bytes 1572868
  22.2 87.9 %copy-start.10 = (u32[32]{0:T(128)S(1)}, u32[32]{0:T(128)}, u32[]{:S(2)}) copy-start(u32[32]{0:T(128)} %constant.76) | copy-start | bytes 388
  22.2 89.3 %copy-start.8 = (f32[16]{0:T(128)S(1)}, f32[16]{0:T(128)}, u32[]{:S(2)}) copy-start(f32[16]{0:T(128)} %copy-done.7) | copy-start | bytes 196
  24.8 0.8 copy-start.1
  27.2 159.3 %all-gather.5.cloned.1.call-start = ((), (), s32[]{:S(2)}) async-start(), calls=%async_computation | async-start | bytes 1572864 | tf_op jit(solution)/shard_map/all_gather | solution.py:135
  27.3 82.8 %collective-permute-start.2 = (bf16[512,2048]{1,0:T(8,128)(2,1)S(1)}, bf16[512,2048]{1,0:T(8,128)(2,1)}, u32[]{:S(2)}, u32[]{:S(2)}) collective-permute-start(bf16[512,2048]{1,0:T(8,128)(2,1)S(1)} %bitcast.92), channel_id=1, source_target_pairs={{0,2},{2,4},{4,6},{6,0},{1,3},{3,5},{5,7},{7,1},{8,10},{10,12},{12... | collective-permute-start | bytes 6291464 | tf_op jit(solution)/shard_map/ppermute | solution.py:140
  110.1 52.7 %collective-permute-start.3 = (bf16[512,2048]{1,0:T(8,128)(2,1)}, bf16[512,2048]{1,0:T(8,128)(2,1)}, u32[]{:S(2)}, u32[]{:S(2)}) collective-permute-start(bf16[512,2048]{1,0:T(8,128)(2,1)} %collective-permute-done.2), channel_id=1, source_target_pairs={{0,2},{2,4},{4,6},{6,0},{1,3},{3,5},{5,7},{7,1},{8,10},{10,12},{12... | collective-permute-start | bytes 6291464 | tf_op jit(solution)/shard_map/ppermute | solution.py:140
  162.8 50.7 %collective-permute-start.4 = (bf16[512,2048]{1,0:T(8,128)(2,1)}, bf16[512,2048]{1,0:T(8,128)(2,1)}, u32[]{:S(2)}, u32[]{:S(2)}) collective-permute-start(bf16[512,2048]{1,0:T(8,128)(2,1)} %collective-permute-done.3), channel_id=1, source_target_pairs={{0,2},{2,4},{4,6},{6,0},{1,3},{3,5},{5,7},{7,1},{8,10},{10,12},{12... | collective-permute-start | bytes 6291464 | tf_op jit(solution)/shard_map/ppermute | solution.py:140
  166.6 6.3 %copy-start.6 = (f32[1,1024]{1,0:T(1,128)S(1)}, f32[1,1024]{1,0:T(1,128)}, u32[]{:S(2)}) copy-start(f32[1,1024]{1,0:T(1,128)} %param.22) | copy-start | bytes 12292
  186.5 38.4 %collective-permute-start.1 = (bf16[256,2048]{0,1:T(8,128)(2,1)}, bf16[256,2048]{0,1:T(8,128)(2,1)S(1)}, u32[]{:S(2)}, u32[]{:S(2)}) collective-permute-start(bf16[256,2048]{0,1:T(8,128)(2,1)} %all-gather.5.cloned.1.call-done), channel_id=1, source_target_pairs={{0,8},{8,16},{16,24},{24,0},{1,9},{9,17},{17,25},{25,1},{2,10},{10... | collective-permute-start | bytes 3145736 | tf_op jit(solution)/shard_map/ppermute | solution.py:35
Sparse Core Ops, SparseCore 0:
  27.3 80.2 all-gather.6
  175.4 11.0 all-gather.4
